TPU v7x, 32 devices: a whole 2x2x4 slice. The times are simulated.
32 devices in a mesh: groups: 2 (over x), hst: 8 (over z, y), head: 2 (over core).
Axes of the slice: x: 2, y: 2, z: 4, core: 2. Of those that a mesh axis runs over, the one named last changes fastest.
Arguments:
- ctx_query: bfloat16 [3072, 64, 128], P(('groups', 'hst'), 'head'), parts along dimension 0, may hold values from -8 to 8
- ctx_key: bfloat16 [3072, 64, 128], P(('groups', 'hst'), 'head'), parts along dimension 0, may hold values from -8 to 8
- ctx_value: bfloat16 [3072, 64, 128], P(('groups', 'hst'), 'head'), parts along dimension 0, may hold values from -6 to 6
- valid: int32 [16], P(('groups', 'hst')), parts along dimension 0, may hold values from 128 to 192
- tail_query: bfloat16 [128, 64, 128], P(('groups', 'hst'), 'head'), parts along dimension 0, may hold values from -8 to 8
- tail_position: int32 [128], P(('groups', 'hst')), parts along dimension 0, may hold values from 1 to 1536
Outputs:
- ctx_out: bfloat16 [3072, 64, 128], P(('groups', 'hst'), 'head'), parts along dimension 0
- tail_out: bfloat16 [128, 64, 128], P(('groups', 'hst'), 'head'), parts along dimension 0
There are 2 independent parts, one for each index of `groups`. A program takes and returns all parts, laid end to end along the dimension named above; each array names one. Nothing has to cross between parts.
All inputs are finite; a program needn't handle non-finite values.
Results may differ from a plain program's by a relative error of at most 0.0043.
Values may be sent and summed in bfloat16 or wider, within the bound.
No kernel may reach another device: no remote copies, remote signals or barrier semaphores. Data moves between devices by JAX's collectives and lax.ppermute only.
A program may use at most 128 MiB of HBM per device.

v0:
```python
import math
import jax
import jax.numpy as jnp
from jax import lax
from jax.sharding import PartitionSpec as P

ANCHOR = 128


def broadcast(array, axis, root):
    mine = lax.axis_index(axis) == root
    return lax.psum(jnp.where(mine, array, jnp.zeros_like(array)), axis)


def masked_softmax(scores, mask):
    scores = jnp.where(mask, scores, jnp.float32(-1e30))
    peak = jnp.max(scores, axis=-1)
    weights = jnp.where(mask, jnp.exp(scores - peak[..., None]), jnp.float32(0.0))
    return (peak, weights, jnp.sum(weights, axis=-1))


def local(ctx_query, ctx_key, ctx_value, valid, tail_query, tail_position):
    block, heads, width = ctx_query.shape
    scale = 1.0 / math.sqrt(width)
    host = lax.axis_index("hst")
    anchor_key, anchor_value = (
        broadcast(ctx_key[:ANCHOR], "hst", 0),
        broadcast(ctx_value[:ANCHOR], "hst", 0),
    )
    own_count = valid[0]
    keys = jnp.concatenate([anchor_key, ctx_key], 0)
    values = jnp.concatenate([anchor_value, ctx_value], 0)
    rows = jnp.arange(block)[:, None]
    cols = jnp.arange(block)[None, :]
    own_mask = (cols <= rows) & (cols < own_count)
    anchor_mask = jnp.broadcast_to(host != 0, (block, ANCHOR))
    mask = jnp.concatenate([anchor_mask, own_mask], 1)
    scores = jnp.einsum("qhd,khd->hqk", ctx_query, keys, preferred_element_type=jnp.float32) * scale
    peak, weights, total = masked_softmax(scores, mask[None])
    summed = jnp.einsum(
        "hqk,khd->qhd", weights.astype(jnp.bfloat16), values, preferred_element_type=jnp.float32
    )
    ctx_out = (summed / jnp.transpose(total)[:, :, None]).astype(jnp.bfloat16)
    far_key, far_value, far_query = (
        lax.all_to_all(ctx_key, "hst", split_axis=1, concat_axis=0, tiled=True),
        lax.all_to_all(ctx_value, "hst", split_axis=1, concat_axis=0, tiled=True),
        lax.all_to_all(tail_query, "hst", split_axis=1, concat_axis=0, tiled=True),
    )
    counts, positions = (
        lax.all_gather(valid, "hst", axis=0, tiled=True),
        lax.all_gather(tail_position, "hst", axis=0, tiled=True),
    )
    starts = jnp.cumsum(counts) - counts
    slots = jnp.arange(block)
    key_places = (starts[:, None] + slots[None, :]).reshape(-1)
    live = (slots[None, :] < counts[:, None]).reshape(-1)
    row_mask = live[None, :] & (key_places[None, :] < positions[:, None])
    tail_scores = (
        jnp.einsum("rhd,khd->hrk", far_query, far_key, preferred_element_type=jnp.float32) * scale
    )
    tail_peak, tail_weights, tail_total = masked_softmax(tail_scores, row_mask[None])
    tail_summed = jnp.einsum(
        "hrk,khd->rhd", tail_weights, far_value.astype(jnp.float32), precision=lax.Precision.HIGHEST
    )
    result = (tail_summed / jnp.transpose(tail_total)[:, :, None]).astype(jnp.bfloat16)
    tail_out = lax.all_to_all(result, "hst", split_axis=0, concat_axis=1, tiled=True)
    return (ctx_out, tail_out)


def solution(mesh):
    in_specs = (
        P(("groups", "hst"), "head", None),
        P(("groups", "hst"), "head", None),
        P(("groups", "hst"), "head", None),
        P(("groups", "hst")),
        P(("groups", "hst"), "head", None),
        P(("groups", "hst")),
    )
    out_specs = (P(("groups", "hst"), "head", None), P(("groups", "hst"), "head", None))
    return jax.shard_map(local, mesh=mesh, in_specs=in_specs, out_specs=out_specs, check_vma=False)
```

profile of v0, /device:TPU:0, one launch (start us, length us, event | category | flops | bytes accessed | tf_op | source)
XLA Modules:
  0.0 242.4 jit_solution(3953943348192276413)
XLA Ops:
  7.2 0.0 copy-start
  7.2 3.3 %copy.20 = bf16[192,32,128]{2,0,1:T(8,128)(2,1)} copy(bf16[192,32,128]{2,1,0:T(8,128)(2,1)} %param.7) | data formatting | bytes 3145728 | tf_op args[1]
  10.5 7.3 %all-to-all-start.1 = ((bf16[192,32,128]{2,0,1:T(8,128)(2,1)}), bf16[192,32,128]{2,0,1:T(8,128)(2,1)S(1)}, u32[]{:S(2)}, u32[]{:S(2)}) async-start(bf16[192,32,128]{2,0,1:T(8,128)(2,1)} %copy.20), calls=%async_computation.1 | async-start | bytes 3145728 | tf_op jit(solution)/shard_map/all_to_all | solution.py:45
  17.8 3.2 %copy.18 = bf16[192,32,128]{2,0,1:T(8,128)(2,1)} copy(bf16[192,32,128]{2,1,0:T(8,128)(2,1)} %param.8) | data formatting | bytes 3145728 | tf_op args[2]
  20.9 2.3 slice_select_fusion.1
  23.2 31.6 %all-to-all-done.1 = bf16[192,32,128]{2,0,1:T(8,128)(2,1)S(1)} async-done(((bf16[192,32,128]{2,0,1:T(8,128)(2,1)}), bf16[192,32,128]{2,0,1:T(8,128)(2,1)S(1)}, u32[]{:S(2)}, u32[]{:S(2)}) %all-to-all-start.1) | async-done | bytes 1572896 | tf_op jit(solution)/shard_map/all_to_all | solution.py:45
  54.8 4.3 %all-to-all-start.2 = ((bf16[192,32,128]{2,0,1:T(8,128)(2,1)}), bf16[192,32,128]{2,0,1:T(8,128)(2,1)}, u32[]{:S(2)}, u32[]{:S(2)}) async-start(bf16[192,32,128]{2,0,1:T(8,128)(2,1)} %copy.18), calls=%async_computation.2 | async-start | bytes 3145728 | tf_op jit(solution)/shard_map/all_to_all | solution.py:46
  59.1 0.0 all-reduce.7.cloned.1.call-start
  59.1 2.3 slice_select_fusion
  61.4 0.0 copy-start.6
  61.4 0.0 copy-start.5
  61.4 0.0 copy-start.3
  61.4 0.0 all-reduce.7.cloned.1.call-update
  62.1 0.0 copy-done.6
  62.1 0.6 dynamic-slice
  63.4 0.0 copy-done.5
  63.4 0.2 dynamic-update-slice.1
  63.6 0.8 dynamic-update-slice
  64.4 54.1 %all-reduce.3 = (s32[8]{0:T(128)S(1)}, s32[64]{0:T(128)S(1)}) all-reduce(s32[8]{0:T(128)S(1)} %dynamic-update-slice, s32[64]{0:T(128)S(1)} %dynamic-update-slice.1), channel_id=1, replica_groups=mesh['groups'=2,'hst'=8,'head'=2] {'hst'}, use_global_device_ids=true, to_apply=%add.1 | all-reduce | flops 72 | bytes 576
  118.5 0.2 reduce-window.9
  118.7 0.1 iota_compare_fusion.1
  118.8 0.1 lt.55
  118.8 0.1 iota_add_fusion
  118.9 0.1 add.24
  119.0 0.0 copy-done.3
  119.0 0.7 copy.23
  119.7 0.1 compare_and_fusion
  119.9 68.3 %all-reduce.7.cloned.1.call-done = (bf16[128,32,128]{2,0,1:T(8,128)(2,1)}, bf16[128,32,128]{2,0,1:T(8,128)(2,1)}) async-done(((bf16[128,32,128]{2,0,1:T(8,128)(2,1)}, bf16[128,32,128]{2,0,1:T(8,128)(2,1)}), (bf16[128,32,128]{2,0,1:T(8,128)(2,1)}, bf16[128,32,128]{2,0,1:T(8,128)(2,1)})) %all-reduce.7.cloned.1.call-update) | async-done | bytes 2097168 | tf_op jit(solution)/shard_map/psum | solution.py:12
  188.2 0.0 copy-done
  188.2 6.8 %fusion.9 = f32[32,320,192]{1,2,0:T(8,128)} fusion(bf16[192,32,128]{2,0,1:T(8,128)(2,1)} %copy.20, bf16[128,32,128]{2,0,1:T(8,128)(2,1)} %get-tuple-element.8, bf16[192,32,128]{2,1,0:T(8,128)(2,1)S(1)} %copy-done), kind=kOutput, calls=%fused_computation.13 | convolution fusion | flops 508559360 | bytes 12058624 | tf_op jit(solution)/shard_map/qhd,khd->hqk/dot_general | solution.py:38
  195.0 0.0 all-to-all-done.2
  195.0 3.9 %all-to-all-start = ((bf16[8,32,128]{2,0,1:T(8,128)(2,1)}), bf16[8,32,128]{2,0,1:T(8,128)(2,1)S(1)}, u32[]{:S(2)}, u32[]{:S(2)}) async-start(bf16[8,32,128]{2,0,1:T(8,128)(2,1)} %copy.23), calls=%async_computation | async-start | bytes 131072 | tf_op jit(solution)/shard_map/all_to_all | solution.py:47
  198.9 14.9 %fusion.37 = (f32[32,192]{1,0:T(8,128)S(1)}, bf16[32,192,320]{2,1,0:T(8,128)(2,1)}) fusion(f32[32,320,192]{1,2,0:T(8,128)} %fusion.9, pred[192,320]{1,0:T(8,128)(4,1)S(1)} %concatenate.10), kind=kOutput, calls=%fused_computation.46 | output fusion | flops 15728959 | bytes 11882496 | tf_op jit(solution)/shard_map/sub | solution.py:18
  213.8 1.3 copy.26
  215.1 0.0 copy-start.1
  215.1 2.8 %copy.28 = bf16[192,8,4,128]{3,0,1,2:T(8,128)(2,1)} copy(bf16[192,8,4,128]{3,0,2,1:T(8,128)(2,1)} %bitcast.14) | data formatting | bytes 3145728 | tf_op jit(solution)/shard_map/all_to_all | solution.py:46
  217.9 0.0 all-to-all-done
  217.9 0.0 copy-done.1
  217.9 0.8 fusion.38
  218.6 0.0 copy-start.2
  218.6 0.4 fusion.17
  219.1 1.0 copy-done.2
  220.0 0.0 copy-start.4
  220.0 1.3 fusion.21
  221.4 0.7 copy.29
  222.0 6.0 %all-to-all-start.3 = ((bf16[64,4,128]{2,1,0:T(4,128)(2,1)}), bf16[64,4,128]{2,1,0:T(4,128)(2,1)S(1)}, u32[]{:S(2)}, u32[]{:S(2)}) async-start(bf16[64,4,128]{2,1,0:T(4,128)(2,1)} %copy.29), calls=%async_computation.3 | async-start | bytes 131072 | tf_op jit(solution)/shard_map/all_to_all | solution.py:66
  228.0 0.0 copy-done.4
  228.0 4.2 %fusion.7 = bf16[192,32,128]{2,0,1:T(8,128)(2,1)S(1)} fusion(f32[192,32]{0,1:T(8,128)S(1)} %bitcast.61, bf16[192,32,128]{2,0,1:T(8,128)(2,1)} %copy.18, bf16[128,32,128]{2,0,1:T(8,128)(2,1)S(1)} %copy-done.4, bf16[32,192,320]{2,1,0:T(8,128)(2,1)} %get-tuple-element.11), kind=kOutput, calls=%fused_computation.10 | convolution fusion | flops 510132224 | bytes 8151040 | tf_op jit(solution)/shard_map/hqk,khd->qhd/dot_general | solution.py:40
  232.3 2.2 copy.31
  234.4 0.5 all-to-all-done.3
  234.9 0.7 copy.30
  (6 shorter events, 0.1 us)
Async XLA Ops:
  7.2 181.0 %copy-start = (bf16[192,32,128]{2,1,0:T(8,128)(2,1)S(1)}, bf16[192,32,128]{2,1,0:T(8,128)(2,1)}, u32[]{:S(2)}) copy-start(bf16[192,32,128]{2,1,0:T(8,128)(2,1)} %param.6) | copy-start | bytes 4718596
  10.5 44.3 %all-to-all-start.1 = ((bf16[192,32,128]{2,0,1:T(8,128)(2,1)}), bf16[192,32,128]{2,0,1:T(8,128)(2,1)S(1)}, u32[]{:S(2)}, u32[]{:S(2)}) async-start(bf16[192,32,128]{2,0,1:T(8,128)(2,1)} %copy.20), calls=%async_computation.1 | async-start | bytes 3145728 | tf_op jit(solution)/shard_map/all_to_all | solution.py:45
  54.8 140.2 %all-to-all-start.2 = ((bf16[192,32,128]{2,0,1:T(8,128)(2,1)}), bf16[192,32,128]{2,0,1:T(8,128)(2,1)}, u32[]{:S(2)}, u32[]{:S(2)}) async-start(bf16[192,32,128]{2,0,1:T(8,128)(2,1)} %copy.18), calls=%async_computation.2 | async-start | bytes 3145728 | tf_op jit(solution)/shard_map/all_to_all | solution.py:46
  59.1 129.1 %all-reduce.7.cloned.1.call-start = ((), (), s32[]{:S(2)}) async-start(), calls=%async_computation.4 | async-start | bytes 4194304 | tf_op jit(solution)/shard_map/psum | solution.py:12
  61.4 0.7 copy-start.6
  61.4 2.0 copy-start.5
  61.4 57.6 %copy-start.3 = (bf16[8,32,128]{2,1,0:T(8,128)(2,1)S(1)}, bf16[8,32,128]{2,1,0:T(8,128)(2,1)}, u32[]{:S(2)}) copy-start(bf16[8,32,128]{2,1,0:T(8,128)(2,1)} %param.10) | copy-start | bytes 196612
  195.0 22.9 %all-to-all-start = ((bf16[8,32,128]{2,0,1:T(8,128)(2,1)}), bf16[8,32,128]{2,0,1:T(8,128)(2,1)S(1)}, u32[]{:S(2)}, u32[]{:S(2)}) async-start(bf16[8,32,128]{2,0,1:T(8,128)(2,1)} %copy.23), calls=%async_computation | async-start | bytes 131072 | tf_op jit(solution)/shard_map/all_to_all | solution.py:47
  215.1 2.8 %copy-start.1 = (bf16[192,8,4,128]{3,0,1,2:T(8,128)(2,1)S(1)}, bf16[192,8,4,128]{3,0,1,2:T(8,128)(2,1)}, u32[]{:S(2)}) copy-start(bf16[192,8,4,128]{3,0,1,2:T(8,128)(2,1)} %copy.26) | copy-start | bytes 4718596
  218.6 1.4 copy-start.2
  220.0 8.0 %copy-start.4 = (bf16[128,32,128]{2,0,1:T(8,128)(2,1)S(1)}, bf16[128,32,128]{2,0,1:T(8,128)(2,1)}, u32[]{:S(2)}) copy-start(bf16[128,32,128]{2,0,1:T(8,128)(2,1)} %get-tuple-element.9) | copy-start | bytes 3145732
  222.0 12.9 %all-to-all-start.3 = ((bf16[64,4,128]{2,1,0:T(4,128)(2,1)}), bf16[64,4,128]{2,1,0:T(4,128)(2,1)S(1)}, u32[]{:S(2)}, u32[]{:S(2)}) async-start(bf16[64,4,128]{2,1,0:T(4,128)(2,1)} %copy.29), calls=%async_computation.3 | async-start | bytes 131072 | tf_op jit(solution)/shard_map/all_to_all | solution.py:66
Sparse Core Ops, SparseCore 0:
  63.6 124.5 all-reduce.6
where the time goes:
time: 243 us; the launch traced here: 242 us
  waiting for transfers between devices  100 us (41%)
  blocking collectives  54.1 us (22%)
  starting transfers between devices  21.6 us (9%)
  other arithmetic  20.3 us (8%)
  local copies, waits for them, and re-layouts  17.5 us (7%)
  between operations  15.5 us (6%)
  matrix products  13.1 us (5%)
    psum x1, waiting for transfers between devices, broadcast(): return lax.psum(jnp.where(mine, array, jnp.zeros_like(array)), axis)  68.3 us
    unnamed x1, blocking collectives  54.1 us
    all_to_all x1, waiting for transfers between devices, local(): lax.all_to_all(ctx_key, 'hst', split_axis=1, concat_axis=0, tiled=True)  31.6 us
    sub x1, other arithmetic, masked_softmax(): scores - peak[..., None]  14.9 us
    unnamed x23, local copies, waits for them, and re-layouts  11.9 us
    all_to_all x1, starting transfers between devices, local(): lax.all_to_all(ctx_key, 'hst', split_axis=1, concat_axis=0, tiled=True)  7.31 us
    dot_general x1, matrix products, local(): jnp.einsum('qhd,khd->hqk', ctx_query, keys, preferred_element_type=jnp.fl...  6.84 us
    all_to_all x1, starting transfers between devices, local(): lax.all_to_all(result, 'hst', split_axis=0, concat_axis=1, tiled=True)  6 us
  transfers between devices with their start and end apart: 5, of which 3 were waited for; matrix products, arithmetic and copies ran while one was open for 18% of the time, Pallas kernels for 0%

commit v1 on v0

--- a/solution.py
+++ b/solution.py
@@ -9,7 +9,7 @@
 
 def broadcast(array, axis, root):
     mine = lax.axis_index(axis) == root
-    return lax.psum(jnp.where(mine, array, jnp.zeros_like(array)), axis)
+    return jnp.sum(lax.all_gather(jnp.where(mine, array, jnp.zeros_like(array)), axis), axis=0)
 
 
 def masked_softmax(scores, mask):

time: 243 us -> 368 us (1.51)
  waiting for transfers between devices: 100 us -> 197 us
  blocking collectives: 54.1 us -> 76.6 us
  other arithmetic: 20.3 us -> 29.2 us
    all_gather x0 -> x2, waiting for transfers between devices: none -> 120 us  [broadcast(): lax.all_gather(jnp.where(mine, array, jnp.zeros_like(array)), axis)]
    psum x1 -> x0, waiting for transfers between devices: 68.3 us -> none  [broadcast(): return lax.psum(jnp.where(mine, array, jnp.zeros_like(array)), axis)]
    all_to_all x1, waiting for transfers between devices: 31.6 us -> 67.4 us  [local(): lax.all_to_all(ctx_key, 'hst', split_axis=1, concat_axis=0, tiled=True)]
    unnamed x1, blocking collectives: 54.1 us -> 76.6 us
    reduce_sum x0 -> x2, other arithmetic: none -> 10.5 us  [broadcast(): jnp.sum(lax.all_gather(jnp.where(mine, array, jnp.zeros_like(array)), axi...]
    all_to_all x1, waiting for transfers between devices: 0.51 us -> 6.59 us  [local(): lax.all_to_all(result, 'hst', split_axis=0, concat_axis=1, tiled=True)]
    unnamed x23 -> x25, local copies, waits for them, and re-layouts: 11.9 us -> 11.2 us
  transfers between devices with their start and end apart: 5 -> 6, of which waited for: 3 -> 5; matrix products, arithmetic and copies ran while one was open for 18% -> 7% of each run, Pallas kernels for 0% -> 0%
where the time goes in v1:
time: 368 us; the launch traced here: 367 us
  waiting for transfers between devices  197 us (54%)
  blocking collectives  76.6 us (21%)
  other arithmetic  29.2 us (8%)
  local copies, waits for them, and re-layouts  18.7 us (5%)
  starting transfers between devices  18.6 us (5%)
  between operations  15.5 us (4%)
  matrix products  11.3 us (3%)
    all_gather x2, waiting for transfers between devices, broadcast(): lax.all_gather(jnp.where(mine, array, jnp.zeros_like(array)), axis)  120 us
    unnamed x1, blocking collectives  76.6 us
    all_to_all x1, waiting for transfers between devices, local(): lax.all_to_all(ctx_key, 'hst', split_axis=1, concat_axis=0, tiled=True)  67.4 us
    sub x1, other arithmetic, masked_softmax(): scores - peak[..., None]  13 us
    unnamed x25, local copies, waits for them, and re-layouts  11.2 us
    reduce_sum x2, other arithmetic, broadcast(): jnp.sum(lax.all_gather(jnp.where(mine, array, jnp.zeros_like(array)), axi...  10.5 us
  transfers between devices with their start and end apart: 6, of which 5 were waited for; matrix products, arithmetic and copies ran while one was open for 7% of the time, Pallas kernels for 0%

profile of v1, /device:TPU:0, one launch (start us, length us, event | category | flops | bytes accessed | tf_op | source)
XLA Modules:
  0.0 367.0 jit_solution(4760555891693292444)
XLA Ops:
  7.2 0.0 copy-start
  7.2 0.0 all-gather.7.cloned.1.call-start
  7.2 2.4 slice_select_fusion
  9.6 0.0 all-gather.7.cloned.1.call-update
  9.6 0.0 copy-start.2
  9.7 0.0 all-gather.5.cloned.1.call-start
  9.7 2.4 slice_select_fusion.1
  12.1 0.0 all-gather.5.cloned.1.call-update
  12.1 0.0 copy-done.2
  12.1 1.8 copy.19
  13.9 7.3 %all-to-all-start.1 = ((bf16[192,32,128]{2,0,1:T(8,128)(2,1)}), bf16[192,32,128]{2,0,1:T(8,128)(2,1)S(1)}, u32[]{:S(2)}, u32[]{:S(2)}) async-start(bf16[192,32,128]{2,0,1:T(8,128)(2,1)} %copy.19), calls=%async_computation.1 | async-start | bytes 3145728 | tf_op jit(solution)/shard_map/all_to_all | solution.py:45
  21.2 3.3 copy.17
  24.5 0.0 copy-start.7
  24.5 0.0 copy-start.6
  24.5 0.0 copy-start.5
  24.5 67.4 %all-to-all-done.1 = bf16[192,32,128]{2,0,1:T(8,128)(2,1)S(1)} async-done(((bf16[192,32,128]{2,0,1:T(8,128)(2,1)}), bf16[192,32,128]{2,0,1:T(8,128)(2,1)S(1)}, u32[]{:S(2)}, u32[]{:S(2)}) %all-to-all-start.1) | async-done | bytes 1572896 | tf_op jit(solution)/shard_map/all_to_all | solution.py:45
  91.9 4.3 %all-to-all-start.2 = ((bf16[192,32,128]{2,0,1:T(8,128)(2,1)}), bf16[192,32,128]{2,0,1:T(8,128)(2,1)}, u32[]{:S(2)}, u32[]{:S(2)}) async-start(bf16[192,32,128]{2,0,1:T(8,128)(2,1)} %copy.17), calls=%async_computation.2 | async-start | bytes 3145728 | tf_op jit(solution)/shard_map/all_to_all | solution.py:46
  96.8 0.0 copy-done.7
  96.8 0.6 dynamic-slice
  98.1 0.8 dynamic-update-slice
  98.9 0.0 copy-done.6
  98.9 0.2 dynamic-update-slice.1
  99.1 76.6 %all-reduce.3 = (s32[8]{0:T(128)S(1)}, s32[64]{0:T(128)S(1)}) all-reduce(s32[8]{0:T(128)S(1)} %dynamic-update-slice, s32[64]{0:T(128)S(1)} %dynamic-update-slice.1), channel_id=1, replica_groups=mesh['groups'=2,'hst'=8,'head'=2] {'hst'}, use_global_device_ids=true, to_apply=%add.1 | all-reduce | flops 72 | bytes 576
  175.7 0.2 reduce-window.9
  175.9 0.1 iota_add_fusion
  175.9 0.1 add.20
  176.0 0.1 iota_compare_fusion.1
  176.1 0.1 lt.55
  176.2 0.0 copy-done.5
  176.2 0.7 copy.21
  176.8 0.0 all-to-all-done.2
  176.8 3.4 all-to-all-start
  180.2 0.1 compare_and_fusion
  180.4 1.3 copy.24
  181.7 0.0 copy-start.1
  181.7 2.8 copy.26
  184.5 3.5 all-to-all-done
  188.0 0.0 copy-done.1
  188.0 0.8 fusion.38
  188.7 0.0 copy-start.4
  188.7 0.4 fusion.17
  189.2 1.0 copy-done.4
  190.2 1.3 fusion.21
  191.5 0.7 copy.27
  192.2 3.5 all-to-all-start.3
  195.8 6.6 %all-to-all-done.3 = bf16[64,4,128]{2,1,0:T(4,128)(2,1)S(1)} async-done(((bf16[64,4,128]{2,1,0:T(4,128)(2,1)}), bf16[64,4,128]{2,1,0:T(4,128)(2,1)S(1)}, u32[]{:S(2)}, u32[]{:S(2)}) %all-to-all-start.3) | async-done | bytes 65568 | tf_op jit(solution)/shard_map/all_to_all | solution.py:66
  202.4 0.7 copy.28
  203.0 0.6 all-gather.7.cloned.1.call-done
  203.6 5.2 %reduce_sum.43 = bf16[128,32,128]{2,1,0:T(8,128)(2,1)S(1)} reduce(bf16[8,128,32,128]{3,2,1,0:T(8,128)(2,1)} %bitcast.55, bf16[]{:T(256)} %constant.7.clone.1), dimensions={0}, to_apply=%region_1.2 | reduce | flops 3670016 | bytes 9437186 | tf_op jit(solution)/shard_map/reduce_sum | solution.py:12
  208.9 1.4 copy.18
  210.2 119.0 %all-gather.5.cloned.1.call-done = bf16[1024,32,128]{2,1,0:T(8,128)(2,1)} async-done(((bf16[128,32,128]{2,1,0:T(8,128)(2,1)}), bf16[1024,32,128]{2,1,0:T(8,128)(2,1)}) %all-gather.5.cloned.1.call-update) | async-done | bytes 8388624 | tf_op jit(solution)/shard_map/all_gather | solution.py:12
  329.2 5.2 %reduce_sum.42 = bf16[128,32,128]{2,1,0:T(8,128)(2,1)S(1)} reduce(bf16[8,128,32,128]{3,2,1,0:T(8,128)(2,1)} %bitcast.56, bf16[]{:T(256)} %constant.7.clone.1), dimensions={0}, to_apply=%region_0.1 | reduce | flops 3670016 | bytes 9437186 | tf_op jit(solution)/shard_map/reduce_sum | solution.py:12
  334.5 0.0 copy-start.3
  334.5 0.4 copy.16
  334.9 0.0 copy-done
  334.9 0.8 copy-done.3
  335.7 6.6 %fusion.9 = f32[32,320,192]{1,2,0:T(8,128)} fusion(bf16[192,32,128]{2,0,1:T(8,128)(2,1)} %copy.19, bf16[128,32,128]{2,0,1:T(8,128)(2,1)S(1)} %copy-done.3, bf16[192,32,128]{2,1,0:T(8,128)(2,1)S(1)} %copy-done), kind=kOutput, calls=%fused_computation.13 | convolution fusion | flops 508559360 | bytes 12058624 | tf_op jit(solution)/shard_map/qhd,khd->hqk/dot_general | solution.py:38
  342.3 13.0 %fusion.37 = (f32[32,192]{1,0:T(8,128)S(1)}, bf16[32,192,320]{2,1,0:T(8,128)(2,1)S(1)}) fusion(f32[32,320,192]{1,2,0:T(8,128)} %fusion.9, pred[192,320]{1,0:T(8,128)(4,1)S(1)} %concatenate.10), kind=kOutput, calls=%fused_computation.46 | output fusion | flops 15728959 | bytes 11882496 | tf_op jit(solution)/shard_map/sub | solution.py:18
  355.3 2.7 fusion.7
  358.0 2.2 copy.29
  (6 shorter events, 0.1 us)
Async XLA Ops:
  7.2 327.8 %copy-start = (bf16[192,32,128]{2,1,0:T(8,128)(2,1)S(1)}, bf16[192,32,128]{2,1,0:T(8,128)(2,1)}, u32[]{:S(2)}) copy-start(bf16[192,32,128]{2,1,0:T(8,128)(2,1)} %param.6) | copy-start | bytes 4718596
  7.2 196.4 %all-gather.7.cloned.1.call-start = ((), (), s32[]{:S(2)}) async-start(), calls=%async_computation.5 | async-start | bytes 9437184 | tf_op jit(solution)/shard_map/all_gather | solution.py:12
  9.6 2.5 copy-start.2
  9.7 319.6 %all-gather.5.cloned.1.call-start = ((), (), s32[]{:S(2)}) async-start(), calls=%async_computation.4 | async-start | bytes 9437184 | tf_op jit(solution)/shard_map/all_gather | solution.py:12
  13.9 78.0 %all-to-all-start.1 = ((bf16[192,32,128]{2,0,1:T(8,128)(2,1)}), bf16[192,32,128]{2,0,1:T(8,128)(2,1)S(1)}, u32[]{:S(2)}, u32[]{:S(2)}) async-start(bf16[192,32,128]{2,0,1:T(8,128)(2,1)} %copy.19), calls=%async_computation.1 | async-start | bytes 3145728 | tf_op jit(solution)/shard_map/all_to_all | solution.py:45
  24.5 72.4 %copy-start.7 = (u32[32]{0:T(128)S(1)}, u32[32]{0:T(128)}, u32[]{:S(2)}) copy-start(u32[32]{0:T(128)} %constant.31) | copy-start | bytes 388
  24.5 74.4 %copy-start.6 = (s32[8]{0:T(128)S(1)}, s32[8]{0:T(128)}, u32[]{:S(2)}) copy-start(s32[8]{0:T(128)} %param.11) | copy-start | bytes 100
  24.5 151.7 %copy-start.5 = (bf16[8,32,128]{2,1,0:T(8,128)(2,1)S(1)}, bf16[8,32,128]{2,1,0:T(8,128)(2,1)}, u32[]{:S(2)}) copy-start(bf16[8,32,128]{2,1,0:T(8,128)(2,1)} %param.10) | copy-start | bytes 196612
  91.9 85.0 %all-to-all-start.2 = ((bf16[192,32,128]{2,0,1:T(8,128)(2,1)}), bf16[192,32,128]{2,0,1:T(8,128)(2,1)}, u32[]{:S(2)}, u32[]{:S(2)}) async-start(bf16[192,32,128]{2,0,1:T(8,128)(2,1)} %copy.17), calls=%async_computation.2 | async-start | bytes 3145728 | tf_op jit(solution)/shard_map/all_to_all | solution.py:46
  176.8 11.1 %all-to-all-start = ((bf16[8,32,128]{2,0,1:T(8,128)(2,1)}), bf16[8,32,128]{2,0,1:T(8,128)(2,1)S(1)}, u32[]{:S(2)}, u32[]{:S(2)}) async-start(bf16[8,32,128]{2,0,1:T(8,128)(2,1)} %copy.21), calls=%async_computation | async-start | bytes 131072 | tf_op jit(solution)/shard_map/all_to_all | solution.py:47
  181.7 6.3 %copy-start.1 = (bf16[192,8,4,128]{3,0,1,2:T(8,128)(2,1)S(1)}, bf16[192,8,4,128]{3,0,1,2:T(8,128)(2,1)}, u32[]{:S(2)}) copy-start(bf16[192,8,4,128]{3,0,1,2:T(8,128)(2,1)} %copy.24) | copy-start | bytes 4718596
  188.7 1.4 copy-start.4
  192.2 10.2 %all-to-all-start.3 = ((bf16[64,4,128]{2,1,0:T(4,128)(2,1)}), bf16[64,4,128]{2,1,0:T(4,128)(2,1)S(1)}, u32[]{:S(2)}, u32[]{:S(2)}) async-start(bf16[64,4,128]{2,1,0:T(4,128)(2,1)} %copy.27), calls=%async_computation.3 | async-start | bytes 131072 | tf_op jit(solution)/shard_map/all_to_all | solution.py:66
  334.5 1.2 copy-start.3
Sparse Core Ops, SparseCore 0:
  10.1 193.4 all-gather.6
  205.7 123.4 all-gather.4
